TPU v7x, 32 devices: a whole 2x2x4 slice. The times are simulated.
32 devices in a mesh: pool: 16 (over z, y, x), serve: 2 (over core).
Axes of the slice: x: 2, y: 2, z: 4, core: 2. Of those that a mesh axis runs over, the one named last changes fastest.
Arguments:
- queries: bfloat16 [2, 256, 73728], P('serve', None, 'pool'), may hold values from -16 to 16
- new_latent: bfloat16 [2, 147456], P('serve', 'pool'), may hold values from -8 to 8
- pool: bfloat16 [2, 192, 36864], P('serve', 'pool'), may hold values from -6 to 6
- page_owner: int32 [2, 32], P('serve'), may hold values from 0 to 15, as said below
- page_slot: int32 [2, 32], P('serve'), may hold values from 0 to 10
- new_owner: int32 [2, 4], P('serve'), may hold values from 0 to 15, as said below
- new_slot: int32 [2, 4], P('serve'), may hold values from 0 to 11
- prefix_len: int32 [2], P('serve'), may hold values from 512 to 2048, as said below
- w_uv: bfloat16 [128, 512, 128], P('pool', 'serve'), may hold values from -1 to 1
Outputs:
- attn_out: bfloat16 [2, 256, 16384], P('serve', None, 'pool')
- new_pool: bfloat16 [2, 192, 36864], P('serve', 'pool')
Inputs may be any that keep to these rules, and one draw needn't show every extreme that they name: Within a request the pairs (page_owner, page_slot) differ from one another and from the pairs (new_owner, new_slot); at most 3 entries of a request's table name the same owner, and in every request some owner is named exactly 3 times. `new_owner`: the 4 new pages of a request go to different owners. `prefix_len`: some request has exactly 2048 prefix tokens.
All inputs are finite; a program needn't handle non-finite values.
Results may differ from a plain program's by a relative error of at most 0.0075.
Values may be sent and summed in bfloat16 or wider, within the bound.
A program may use at most 128 MiB of HBM per device.

v0:
```python
import jax
import jax.numpy as jnp
from jax import lax
from jax.sharding import PartitionSpec as P

VLAT = 512
VHEAD = 128
PAGE = 64
SUF = 256
HOT = 3
LAT = 576
PPAGES = 32
NEWP = 4
SLOTS = 12


softmax_scale = 192.0 ** (-0.5)
masked_score = -1e30


def absorb(running, query_rows, key_rows, allowed):
    top_old, sum_old, mixture_old = running
    scores = (
        jnp.einsum("qhd,kd->hqk", query_rows, key_rows, preferred_element_type=jnp.float32)
        * softmax_scale
    )
    scores = jnp.where(allowed, scores, masked_score)
    top_score = jnp.maximum(top_old, jnp.max(scores, axis=-1))
    rescale = jnp.exp(top_old - top_score)
    weights = jnp.exp(scores - top_score[..., None])
    weight_sum = sum_old * rescale + jnp.sum(weights, axis=-1)
    mixture = mixture_old * rescale[..., None] + jnp.einsum(
        "hqk,kv->hqv",
        weights.astype(jnp.bfloat16),
        key_rows[:, :VLAT],
        preferred_element_type=jnp.float32,
    )
    return (top_score, weight_sum, mixture)


def local(queries, new_latent, pool, page_owner, page_slot, new_owner, new_slot, prefix_len, w_uv):
    holder = lax.axis_index("pool")
    head_count = queries.shape[2] // LAT
    query_rows = queries.reshape(SUF, head_count, LAT)
    suffix_all = lax.all_gather(new_latent, "pool", axis=1, tiled=True)
    suffix = suffix_all.reshape(SUF, LAT)
    position = jnp.arange(SUF, dtype=jnp.int32)
    causal = position[None, :] <= position[:, None]
    start_state = (
        jnp.full((head_count, SUF), masked_score, jnp.float32),
        jnp.zeros((head_count, SUF), jnp.float32),
        jnp.zeros((head_count, SUF, VLAT), jnp.float32),
    )
    running = absorb(start_state, query_rows, suffix, causal[None])
    owners = page_owner[0]
    slot_ids = page_slot[0]
    length = prefix_len[0]
    page_index = jnp.arange(PPAGES, dtype=jnp.int32)
    tokens = jnp.clip(length - PAGE * page_index, 0, PAGE)
    local_pages = pool[0]
    block_pages = max(1, 512 // PAGE)
    earlier = (page_index[None, :] < page_index[:, None]) & (owners[None, :] == owners[:, None])
    rank_among = jnp.sum(earlier.astype(jnp.int32), axis=1)
    gathered_row = owners * HOT + rank_among
    my_ranks = jnp.arange(HOT, dtype=jnp.int32)
    my_rows = (owners[None, :] == holder) & (rank_among[None, :] == my_ranks[:, None])
    slot_rows = jnp.sum(jnp.where(my_rows, slot_ids[None, :], 0), axis=1)
    outgoing = local_pages[slot_rows]
    gathered = lax.all_gather(outgoing, "pool", axis=0, tiled=True)
    prefix_pages = gathered[gathered_row]
    for opening in range(0, PPAGES, block_pages):
        closing = min(PPAGES, opening + block_pages)
        key_rows = prefix_pages[opening:closing].reshape(-1, LAT)
        inside = (
            lax.broadcasted_iota(jnp.int32, (closing - opening, PAGE), 1)
            < tokens[opening:closing, None]
        ).reshape(-1)
        running = absorb(running, query_rows, key_rows, inside[None, None, :])
    latent_out = (running[2] / running[1][..., None]).astype(jnp.bfloat16)
    projected = jnp.einsum(
        "hqv,hve->qhe",
        latent_out,
        lax.all_gather(w_uv, "serve", axis=1, tiled=True),
        preferred_element_type=jnp.float32,
    )
    attended = projected.astype(jnp.bfloat16).reshape(1, SUF, head_count * VHEAD)
    fresh_pages = suffix_all.reshape(NEWP, PAGE * LAT)
    placing = (jnp.arange(SLOTS, dtype=jnp.int32)[:, None] == new_slot[0][None, :]) & (
        new_owner[0][None, :] == holder
    )
    written = jnp.dot(
        placing.astype(jnp.bfloat16), fresh_pages, preferred_element_type=jnp.float32
    ).astype(jnp.bfloat16)
    updated = jnp.where(jnp.any(placing, axis=1)[:, None], written, local_pages)
    return (attended, updated[None])


def solution(mesh):
    in_specs = (
        P("serve", None, "pool"),
        P("serve", "pool"),
        P("serve", "pool", None),
        P("serve", None),
        P("serve", None),
        P("serve", None),
        P("serve", None),
        P("serve"),
        P("pool", "serve", None),
    )
    out_specs = (P("serve", None, "pool"), P("serve", "pool", None))
    return jax.shard_map(local, mesh=mesh, in_specs=in_specs, out_specs=out_specs, check_vma=False)
```

profile of v0, /device:TPU:16, one launch (start us, length us, event | category | flops | bytes accessed | tf_op | source)
XLA Modules:
  0.0 158.7 jit_solution(11792393824957913904)
XLA Ops:
  7.2 0.0 copy-start.13
  7.2 0.0 copy-start.8
  7.2 0.0 all-gather.7.cloned.1.call-start
  7.2 0.7 compare_bitcast_fusion.1
  7.9 0.9 convert_reduce_fusion
  8.8 0.8 select_reduce_fusion
  9.6 3.1 %gather_fusion = bf16[3,36864]{1,0:T(4,128)(2,1)} fusion(bf16[12,36864]{1,0:T(8,128)(2,1)} %bitcast.124, s32[1024]{0:T(1024)S(1)} %pad_clamp_fusion.1), kind=kCustom, calls=%fused_computation | custom fusion | bytes 442380 | tf_op jit(solution)/shard_map/gather | solution.py:68
  12.7 0.0 all-gather.7.cloned.1.call-update
  12.7 0.0 all-gather.5.cloned.1.call-start
  12.8 2.0 %copy.50 = bf16[8,256,128]{1,2,0:T(8,128)(2,1)} copy(bf16[8,256,128]{2,1,0:T(8,128)(2,1)} %param.17) | data formatting | bytes 1048576 | tf_op args[8]
  14.8 0.0 all-gather.5.cloned.1.call-update
  14.9 0.0 copy-done.13
  14.9 0.6 iota_compare_fusion
  15.5 37.7 %all_gather.9 = bf16[1,147456]{1,0:T(2,128)(2,1)S(1)} all-gather(bf16[1,9216]{1,0:T(2,128)(2,1)S(1)} %copy-done.8), channel_id=1, replica_groups=mesh['pool'=16,'serve'=2] {'pool'}, dimensions={1}, use_global_device_ids=true | all-gather | bytes 313344 | tf_op jit(solution)/shard_map/all_gather | solution.py:45
  53.2 6.1 %reduce = bf16[147456]{0:T(1024)(128)(2,1)S(1)} reduce(bf16[1,147456]{1,0:T(2,128)(2,1)S(1)} %all_gather.9, bf16[]{:T(256)} %constant.42), dimensions={0}, to_apply=%all_gather.9.reduce_sub_computation | reduce | bytes 589826 | tf_op jit(solution)/shard_map/all_gather | solution.py:45
  59.3 1.0 reshape.249
  60.3 0.8 reshape.256
  61.8 0.5 fusion.80
  62.3 0.1 iota_compare_fusion.3
  62.4 0.7 lt.107
  63.1 2.8 %copy.39 = bf16[1,256,4608]{1,2,0:T(8,128)(2,1)S(1)} copy(bf16[1,256,4608]{2,1,0:T(8,128)(2,1)} %param.9) | data formatting | bytes 4718592 | tf_op args[0]
  65.9 0.7 lt.104
  66.7 0.1 iota_compare_fusion.2
  66.7 0.1 lt.110
  66.8 0.1 iota_compare_fusion.5
  66.9 0.6 lt.96
  67.5 0.7 compare_bitcast_fusion
  68.2 0.7 fusion.61
  68.9 2.7 %fusion.1 = bf16[1,12,36864]{2,1,0:T(8,128)(2,1)} fusion(bf16[4,36864]{1,0:T(4,128)(2,1)} %reshape.256, pred[12]{0:T(512)(128)(4,1)S(1)} %fusion.61, s32[4]{0:T(128)} %bitcast.134, pred[4]{0:T(512)(128)(4,1)S(1)} %compare_bitcast_fusion, bf16[1,12,36864]{2,1,0:T(8,128)(2,1)S(1)} %copy-done), kind=kOutput, calls=%fused_computation.4 | convolution fusion | flops 4423776 | bytes 2064416 | tf_op jit(solution)/shard_map/dot_general | solution.py:91
  71.6 3.4 %fusion.81 = (f32[8,256]{1,0:T(8,128)S(1)}, f32[8,256,256]{1,2,0:T(8,128)}) fusion(bf16[256,8,576]{0,2,1:T(8,128)(2,1)S(1)} %bitcast.125, bf16[256,576]{1,0:T(8,128)(2,1)} %reshape.249, pred[256,256]{0,1:T(8,128)(4,1)} %iota_compare_fusion), kind=kOutput, calls=%fused_computation.116 | convolution fusion | flops 605550592 | bytes 4825088 | tf_op jit(solution)/shard_map/qhd,kd->hqk/dot_general | solution.py:24
  75.0 22.8 %all-gather.7.cloned.1.call-done = bf16[16,3,36864]{2,1,0:T(4,128)(2,1)} async-done(((bf16[1,3,36864]{2,1,0:T(4,128)(2,1)}), bf16[16,3,36864]{2,1,0:T(4,128)(2,1)}) %all-gather.7.cloned.1.call-update) | async-done | bytes 3538960 | tf_op jit(solution)/shard_map/all_gather | solution.py:69
  97.8 4.8 %reshape.275 = bf16[48,36864]{1,0:T(8,128)(2,1)S(1)} reshape(bf16[16,3,36864]{2,1,0:T(4,128)(2,1)} %all-gather.7.cloned.1.call-done) | data formatting | bytes 7077888
  102.6 3.5 %gather_fusion.1 = bf16[32,36864]{1,0:T(8,128)(2,1)} fusion(bf16[48,36864]{1,0:T(8,128)(2,1)S(1)} %reshape.275, s32[1024]{0:T(1024)S(1)} %pad_clamp_fusion), kind=kCustom, calls=%fused_computation.1 | custom fusion | bytes 4718720 | tf_op jit(solution)/shard_map/gather | solution.py:70
  106.1 2.0 %fusion.79 = (bf16[8,36864]{1,0:T(8,128)(2,1)S(1)}, bf16[8,36864]{1,0:T(8,128)(2,1)S(1)}, bf16[8,36864]{1,0:T(8,128)(2,1)S(1)}, bf16[8,36864]{1,0:T(8,128)(2,1)S(1)}) fusion(bf16[32,36864]{1,0:T(8,128)(2,1)} %gather_fusion.1), kind=kLoop, calls=%fused_computation.114 | loop fusion | bytes 4718592 | tf_op jit(solution)/shard_map/slice | solution.py:73
  108.1 0.8 reshape.253
  108.9 1.6 %reshape.252 = bf16[512,576]{1,0:T(8,128)(2,1)} reshape(bf16[8,36864]{1,0:T(8,128)(2,1)S(1)} %get-tuple-element.21) | data formatting | bytes 1179648 | tf_op jit(solution)/shard_map/reshape | solution.py:73
  110.5 0.8 reshape.254
  111.3 1.6 %reshape.251 = bf16[512,576]{1,0:T(8,128)(2,1)} reshape(bf16[8,36864]{1,0:T(8,128)(2,1)S(1)} %get-tuple-element.19) | data formatting | bytes 1179648 | tf_op jit(solution)/shard_map/reshape | solution.py:73
  113.0 0.0 copy-done.9
  113.0 3.7 %bitcast_reduce_fusion.1 = (f32[8,256]{1,0:T(8,128)S(1)}, f32[512,256,8]{1,0,2:T(8,128)S(1)}) fusion(pred[512]{0:T(512)(128)(4,1)S(1)} %copy-done.9, bf16[256,8,576]{0,2,1:T(8,128)(2,1)} %bitcast.126, bf16[512,576]{1,0:T(8,128)(2,1)S(1)} %reshape.253), kind=kOutput, calls=%fused_computation.9 | convolution fusion | flops 1211103232 | bytes 7152128 | tf_op jit(solution)/shard_map/qhd,kd->hqk/dot_general | solution.py:24
  116.7 0.0 copy-done.4
  116.7 0.0 copy-done.6
  116.7 0.0 copy-done.10
  116.7 1.9 %bitcast_reduce_fusion.2 = (f32[8,256]{1,0:T(8,128)S(1)}, f32[512,256,8]{1,0,2:T(8,128)S(1)}) fusion(pred[512]{0:T(512)(128)(4,1)S(1)} %copy-done.10, bf16[256,8,576]{0,2,1:T(8,128)(2,1)S(1)} %bitcast.127, bf16[512,576]{1,0:T(8,128)(2,1)S(1)} %copy-done.6), kind=kOutput, calls=%fused_computation.12 | convolution fusion | flops 1211103232 | bytes 7152128 | tf_op jit(solution)/shard_map/qhd,kd->hqk/dot_general | solution.py:24
  118.6 1.9 %bitcast_reduce_fusion = (f32[8,256]{1,0:T(8,128)S(1)}, f32[512,256,8]{1,0,2:T(8,128)S(1)}) fusion(pred[512]{0:T(512)(128)(4,1)S(1)} %lt.110, bf16[256,8,576]{0,2,1:T(8,128)(2,1)S(1)} %bitcast.128, bf16[512,576]{1,0:T(8,128)(2,1)S(1)} %reshape.254), kind=kOutput, calls=%fused_computation.6 | convolution fusion | flops 1211103232 | bytes 7152128 | tf_op jit(solution)/shard_map/qhd,kd->hqk/dot_general | solution.py:24
  120.5 0.0 copy-done.7
  120.5 0.0 copy-done.11
  120.6 0.0 copy-start.2
  120.6 1.9 %bitcast_reduce_fusion.3 = (f32[8,256]{1,0:T(8,128)S(1)}, f32[512,256,8]{1,0,2:T(8,128)S(1)}) fusion(pred[512]{0:T(512)(128)(4,1)S(1)} %copy-done.11, bf16[256,8,576]{0,2,1:T(8,128)(2,1)S(1)} %bitcast.129, bf16[512,576]{1,0:T(8,128)(2,1)S(1)} %copy-done.7), kind=kOutput, calls=%fused_computation.15 | convolution fusion | flops 1211103232 | bytes 7152128 | tf_op jit(solution)/shard_map/qhd,kd->hqk/dot_general | solution.py:24
  122.5 0.9 fusion.6
  123.4 0.0 copy-start.1
  123.4 0.0 copy-start.5
  123.4 3.6 %fusion.19 = f32[8,256,512]{2,1,0:T(8,128)} fusion(f32[512,256,8]{1,0,2:T(8,128)S(1)} %get-tuple-element.36, f32[8,256]{1,0:T(8,128)S(1)} %get-tuple-element.18, pred[512]{0:T(512)(128)(4,1)S(1)} %copy-done.11, bf16[512,576]{1,0:T(8,128)(2,1)S(1)} %copy-done.7), kind=kOutput, calls=%fused_computation.32 | convolution fusion | flops 1077936128 | bytes 8921600 | tf_op jit(solution)/shard_map/hqk,kv->hqv/dot_general | solution.py:32
  127.0 0.3 fusion.37
  127.3 0.0 copy-done.5
  127.3 2.9 %fusion.45 = f32[8,256,512]{2,1,0:T(8,128)} fusion(f32[8,256,256]{1,2,0:T(8,128)S(1)} %copy-done.1, f32[8,256]{1,0:T(8,128)S(1)} %get-tuple-element.24, bf16[256,576]{1,0:T(8,128)(2,1)S(1)} %copy-done.5), kind=kOutput, calls=%fused_computation.55 | convolution fusion | flops 537919488 | bytes 6561792 | tf_op jit(solution)/shard_map/hqk,kv->hqv/dot_general | solution.py:32
  130.2 0.9 fusion.10
  131.2 0.9 fusion.8
  132.1 0.0 copy-done.2
  132.1 0.9 fusion.12
  133.0 3.6 %fusion.17 = f32[8,256,512]{2,1,0:T(8,128)} fusion(f32[512,256,8]{1,0,2:T(8,128)S(1)} %get-tuple-element.34, f32[8,256]{1,0:T(8,128)S(1)} %get-tuple-element.17, pred[512]{0:T(512)(128)(4,1)S(1)} %copy-done.10, bf16[512,576]{1,0:T(8,128)(2,1)S(1)} %copy-done.6), kind=kOutput, calls=%fused_computation.31 | convolution fusion | flops 1077936128 | bytes 8921600 | tf_op jit(solution)/shard_map/hqk,kv->hqv/dot_general | solution.py:32
  136.6 3.6 %fusion.15 = f32[8,256,512]{2,1,0:T(8,128)} fusion(f32[512,256,8]{1,0,2:T(8,128)S(1)} %get-tuple-element.32, f32[8,256]{1,0:T(8,128)S(1)} %get-tuple-element.16, pred[512]{0:T(512)(128)(4,1)S(1)} %copy-done.9, bf16[512,576]{1,0:T(8,128)(2,1)S(1)} %reshape.253), kind=kOutput, calls=%fused_computation.30 | convolution fusion | flops 1077936128 | bytes 8921600 | tf_op jit(solution)/shard_map/hqk,kv->hqv/dot_general | solution.py:32
  140.2 10.7 %fusion.42 = bf16[8,256,128]{1,2,0:T(8,128)(2,1)S(1)} fusion(bf16[8,512,128]{1,2,0:T(8,128)(2,1)} %all-gather.5.cloned.1.call-done, f32[8,256,512]{2,1,0:T(8,128)} %fusion.15, f32[8,256,512]{2,1,0:T(8,128)} %fusion.17, f32[8,256,512]{2,1,0:T(8,128)} %fusion.19, f32[8,256,512]{2,1,0:T(8,128)} %fusion.45, f32[512,256,8]{1,0,2:T(8,128)} %copy-done.2, ...), kind=kOutput, calls=%fused_computation.54 | convolution fusion | flops 1358168064 | bytes 23126528 | tf_op jit(solution)/shard_map/hqv,hve->qhe/dot_general | solution.py:80
  150.9 1.0 copy.51
  (22 shorter events, 0.1 us)
Async XLA Ops:
  7.2 7.7 %copy-start.13 = (s32[1,32]{1,0:T(1,128)S(1)}, s32[1,32]{1,0:T(1,128)}, u32[]{:S(2)}) copy-start(s32[1,32]{1,0:T(1,128)} %param.12) | copy-start | bytes 388
  7.2 8.4 %copy-start.8 = (bf16[1,9216]{1,0:T(2,128)(2,1)S(1)}, bf16[1,9216]{1,0:T(2,128)(2,1)}, u32[]{:S(2)}) copy-start(bf16[1,9216]{1,0:T(2,128)(2,1)} %param.10) | copy-start | bytes 55300
  7.2 90.6 %all-gather.7.cloned.1.call-start = ((), (), s32[]{:S(2)}) async-start(), calls=%async_computation.1 | async-start | bytes 5013504 | tf_op jit(solution)/shard_map/all_gather | solution.py:69
  12.7 127.5 %all-gather.5.cloned.1.call-start = ((), (), s32[]{:S(2)}) async-start(), calls=%async_computation | async-start | bytes 1572864 | tf_op jit(solution)/shard_map/all_gather | solution.py:83
  14.8 54.1 %copy-start = (bf16[1,12,36864]{2,1,0:T(8,128)(2,1)S(1)}, bf16[1,12,36864]{2,1,0:T(8,128)(2,1)}, u32[]{:S(2)}) copy-start(bf16[1,12,36864]{2,1,0:T(8,128)(2,1)} %param.11) | copy-start | bytes 2654212
  63.1 3.8 %copy-start.12 = (s32[8]{0:T(128)S(1)}, s32[8]{0:T(128)}, u32[]{:S(2)}) copy-start(s32[8]{0:T(128)} %get-tuple-element.25) | copy-start | bytes 100
  65.9 9.1 %copy-start.3 = (bf16[1,256,4608]{1,2,0:T(8,128)(2,1)}, bf16[1,256,4608]{1,2,0:T(8,128)(2,1)S(1)}, u32[]{:S(2)}) copy-start(bf16[1,256,4608]{1,2,0:T(8,128)(2,1)S(1)} %copy.39) | copy-start | bytes 7077892
  106.1 6.9 %copy-start.9 = (pred[512]{0:T(512)(128)(4,1)S(1)}, pred[512]{0:T(512)(128)(4,1)}, u32[]{:S(2)}) copy-start(pred[512]{0:T(512)(128)(4,1)} %lt.107) | copy-start | bytes 1540
  113.0 3.7 %copy-start.4 = (bf16[1,256,4608]{1,2,0:T(8,128)(2,1)S(1)}, bf16[1,256,4608]{1,2,0:T(8,128)(2,1)}, u32[]{:S(2)}) copy-start(bf16[1,256,4608]{1,2,0:T(8,128)(2,1)} %copy-done.3) | copy-start | bytes 7077892
  113.0 3.7 %copy-start.6 = (bf16[512,576]{1,0:T(8,128)(2,1)S(1)}, bf16[512,576]{1,0:T(8,128)(2,1)}, u32[]{:S(2)}) copy-start(bf16[512,576]{1,0:T(8,128)(2,1)} %reshape.252) | copy-start | bytes 1769476
  113.0 3.7 %copy-start.10 = (pred[512]{0:T(512)(128)(4,1)S(1)}, pred[512]{0:T(512)(128)(4,1)}, u32[]{:S(2)}) copy-start(pred[512]{0:T(512)(128)(4,1)} %lt.104) | copy-start | bytes 1540
  118.6 1.9 %copy-start.7 = (bf16[512,576]{1,0:T(8,128)(2,1)S(1)}, bf16[512,576]{1,0:T(8,128)(2,1)}, u32[]{:S(2)}) copy-start(bf16[512,576]{1,0:T(8,128)(2,1)} %reshape.251) | copy-start | bytes 1769476
  118.6 1.9 %copy-start.11 = (pred[512]{0:T(512)(128)(4,1)S(1)}, pred[512]{0:T(512)(128)(4,1)}, u32[]{:S(2)}) copy-start(pred[512]{0:T(512)(128)(4,1)} %lt.96) | copy-start | bytes 1540
  120.6 11.5 %copy-start.2 = (f32[512,256,8]{1,0,2:T(8,128)}, f32[512,256,8]{1,0,2:T(8,128)S(1)}, u32[]{:S(2)}) copy-start(f32[512,256,8]{1,0,2:T(8,128)S(1)} %get-tuple-element.30) | copy-start | bytes 12582916
  123.4 3.6 %copy-start.1 = (f32[8,256,256]{1,2,0:T(8,128)S(1)}, f32[8,256,256]{1,2,0:T(8,128)}, u32[]{:S(2)}) copy-start(f32[8,256,256]{1,2,0:T(8,128)} %get-tuple-element.38) | copy-start | bytes 6291460
  123.4 3.9 %copy-start.5 = (bf16[256,576]{1,0:T(8,128)(2,1)S(1)}, bf16[256,576]{1,0:T(8,128)(2,1)}, u32[]{:S(2)}) copy-start(bf16[256,576]{1,0:T(8,128)(2,1)} %reshape.249) | copy-start | bytes 884740
Sparse Core Ops, SparseCore 0:
  12.9 84.8 all-gather.6
  99.9 8.1 all-gather.4
where the time goes:
time: 161 us; the launch traced here: 159 us
  matrix products  39.7 us (25%)
  blocking collectives  37.7 us (23%)
  local copies, waits for them, and re-layouts  28.6 us (18%)
  waiting for transfers between devices  22.8 us (14%)
  between operations  15 us (9%)
  other arithmetic  14.8 us (9%)
    all_gather x1, blocking collectives, local(): suffix_all = lax.all_gather(new_latent, 'pool', axis=1, tiled=True)  37.7 us
    all_gather x1, waiting for transfers between devices, local(): gathered = lax.all_gather(outgoing, 'pool', axis=0, tiled=True)  22.8 us
    dot_general x4, matrix products, absorb(): jnp.einsum('hqk,kv->hqv', weights.astype(jnp.bfloat16), key_rows[:, :VLAT...  13.7 us
    dot_general x5, matrix products, absorb(): jnp.einsum('qhd,kd->hqk', query_rows, key_rows, preferred_element_type=jn...  12.8 us
    unnamed x32, local copies, waits for them, and re-layouts  10.7 us
    dot_general x1, matrix products, local(): jnp.einsum('hqv,hve->qhe', latent_out, lax.all_gather(w_uv, 'serve', axis...  10.7 us
    all_gather x1, other arithmetic, local(): suffix_all = lax.all_gather(new_latent, 'pool', axis=1, tiled=True)  6.11 us
    reshape x4, local copies, waits for them, and re-layouts, local(): key_rows = prefix_pages[opening:closing].reshape(-1, LAT)  4.88 us
  transfers between devices with their start and end apart: 2, of which 1 were waited for; matrix products, arithmetic and copies ran while one was open for 42% of the time, Pallas kernels for 0%

commit v1 on v0

v1 whole, which is shorter than its diff:
```python
import functools

import jax
import jax.numpy as jnp
from jax import lax
from jax.experimental import pallas as pl
from jax.experimental.pallas import tpu as pltpu
from jax.sharding import PartitionSpec as P

VLAT = 512
VHEAD = 128
PAGE = 64
SUF = 256
HOT = 3
LAT = 576
PPAGES = 32
NEWP = 4
SLOTS = 12

LANES = 128
ROPE = LAT - VLAT
PAGE_ROWS = PAGE * LAT // LANES
KEYS = PPAGES * PAGE + SUF
WIDE = 640

softmax_scale = 192.0 ** (-0.5)
masked_score = -1e30
exp2_scale = softmax_scale * 1.4426950408889634

MESH = pl.DeviceIdType.MESH


def exchange_kernel(n, serve_n, block_ref, w_ref, g_ref, wg_ref,
                    z_send, z_recv, x_send, x_recv, y_send, y_recv, w_send, w_recv):
    depth = n // 4
    me = lax.axis_index("pool")
    core = lax.axis_index("serve")
    x = me % 2
    y = (me // 2) % 2
    z = me // 4
    x_peer = z * 4 + y * 2 + (1 - x)
    y_peer = z * 4 + (1 - y) * 2 + x

    barrier = pltpu.get_barrier_semaphore()
    for d in range(1, depth):
        there = ((z + d) % depth) * 4 + y * 2 + x
        pl.semaphore_signal(barrier, inc=1, device_id={"pool": there}, device_id_type=MESH)
    pl.semaphore_signal(barrier, inc=1, device_id={"pool": x_peer}, device_id_type=MESH)
    pl.semaphore_signal(barrier, inc=1, device_id={"pool": y_peer}, device_id_type=MESH)
    for d in range(1, serve_n):
        pl.semaphore_signal(
            barrier, inc=1, device_id={"serve": (core + d) % serve_n}, device_id_type=MESH
        )
    pl.semaphore_wait(barrier, depth + serve_n)

    started = []

    def send(src, dst, send_sem, recv_sem, device_id):
        copy = pltpu.make_async_remote_copy(
            src_ref=src, dst_ref=dst, send_sem=send_sem, recv_sem=recv_sem,
            device_id=device_id, device_id_type=MESH,
        )
        copy.start()
        started.append(copy)
        return copy

    order = []
    for d in range(1, depth // 2 + 1):
        order.append(d)
        if depth - d != d:
            order.append(depth - d)

    def spread(d):
        owner = ((z - d + depth) % depth) * 4 + y * 2 + x
        src = block_ref if d == 0 else g_ref.at[owner]
        x_first = send(src.at[0], g_ref.at[owner, 0], x_send.at[d, 0], x_recv.at[d, 0], {"pool": x_peer})
        y_first = send(src.at[1], g_ref.at[owner, 1], y_send.at[d, 0], y_recv.at[d, 0], {"pool": y_peer})
        x_second = send(src.at[1], g_ref.at[owner, 1], x_send.at[d, 1], x_recv.at[d, 1], {"pool": x_peer})
        y_second = send(src.at[0], g_ref.at[owner, 0], y_send.at[d, 1], y_recv.at[d, 1], {"pool": y_peer})
        return x_first, y_first, x_second, y_second

    waits = []

    def forward(d, copies):
        x_first, y_first, x_second, y_second = copies
        base = ((z - d + depth) % depth) * 4
        x_first.wait_recv()
        from_x = base + y * 2 + (1 - x)
        waits.append(send(g_ref.at[from_x, 0], g_ref.at[from_x, 0],
                          y_send.at[d, 2], y_recv.at[d, 2], {"pool": y_peer}))
        y_first.wait_recv()
        from_y = base + (1 - y) * 2 + x
        waits.append(send(g_ref.at[from_y, 1], g_ref.at[from_y, 1],
                          x_send.at[d, 2], x_recv.at[d, 2], {"pool": x_peer}))
        waits.append(x_second)
        waits.append(y_second)

    z_copies = {}
    prior = None
    first = spread(0)
    for d in order:
        there = ((z + d) % depth) * 4 + y * 2 + x
        z_copies[d] = send(block_ref, g_ref.at[me], z_send.at[d], z_recv.at[d], {"pool": there})
    for d in range(1, serve_n):
        waits.append(send(w_ref, wg_ref.at[core], w_send.at[d], w_recv.at[d],
                          {"serve": (core + d) % serve_n}))
    g_ref[pl.ds(me, 1)] = block_ref[...][None]
    wg_ref[pl.ds(core, 1)] = w_ref[...][None]
    prior = (0, first)
    for d in order:
        z_copies[d].wait_recv()
        now = spread(d)
        forward(*prior)
        prior = (d, now)
    forward(*prior)
    for copy in waits:
        copy.wait_recv()
    for copy in started:
        copy.wait_send()


def exchange(n, serve_n, block, w):
    depth = n // 4
    dma = pltpu.SemaphoreType.DMA
    vmem = pl.BlockSpec(memory_space=pltpu.VMEM)
    return pl.pallas_call(
        functools.partial(exchange_kernel, n, serve_n),
        out_shape=(
            jax.ShapeDtypeStruct((n,) + block.shape, block.dtype),
            jax.ShapeDtypeStruct((serve_n,) + w.shape, w.dtype),
        ),
        in_specs=[vmem, vmem],
        out_specs=(vmem, vmem),
        scratch_shapes=[
            dma((depth,)), dma((depth,)),
            dma((depth, 3)), dma((depth, 3)),
            dma((depth, 3)), dma((depth, 3)),
            dma((serve_n,)), dma((serve_n,)),
        ],
        compiler_params=pltpu.CompilerParams(
            collective_id=0, has_side_effects=True, vmem_limit_bytes=24 * 1024 * 1024
        ),
        name="exchange",
    )(block, w)


def attend_kernel(block_rows, owner_ref, rank_ref, length_ref, q_ref, g_ref, suffix_ref, wg_ref,
                  out_ref, keys_ref, bias_ref, causal_ref):
    @pl.when(pl.program_id(0) == 0)
    def _():
        def place(j, carry):
            base = pl.multiple_of(owner_ref[j] * block_rows + rank_ref[j] * PAGE_ROWS, 16)
            row = pl.multiple_of(j * PAGE, PAGE)
            for c in range(VLAT // LANES):
                keys_ref[pl.ds(row, PAGE), c * LANES:(c + 1) * LANES] = g_ref[pl.ds(base + c * PAGE, PAGE), :]
            rope = g_ref[pl.ds(base + PAGE * VLAT // LANES, PAGE // 2), :]
            keys_ref[pl.ds(row, PAGE // 2), VLAT:WIDE] = rope
            keys_ref[pl.ds(row + PAGE // 2, PAGE // 2), VLAT:WIDE] = jnp.concatenate(
                [rope[:, ROPE:], rope[:, :ROPE]], axis=1
            )
            return carry

        lax.fori_loop(0, PPAGES, place, 0)
        keys_ref[PPAGES * PAGE:, :] = suffix_ref[...]
        spot = lax.broadcasted_iota(jnp.int32, (8, PPAGES * PAGE), 1)
        bias_ref[...] = jnp.where(spot < length_ref[0], 0.0, masked_score)
        row = lax.broadcasted_iota(jnp.int32, (SUF, SUF), 0)
        col = lax.broadcasted_iota(jnp.int32, (SUF, SUF), 1)
        causal_ref[...] = jnp.where(col <= row, 0.0, masked_score)

    prefix = PPAGES * PAGE
    zeros = jnp.zeros((SUF, WIDE - LAT), jnp.bfloat16)
    contract_last = (((1,), (1,)), ((), ()))
    for h in range(2):
        q = jnp.concatenate([q_ref[:, h * LAT:(h + 1) * LAT], zeros], axis=1)
        s_suffix = lax.dot_general(
            q, keys_ref[prefix:, :], contract_last, preferred_element_type=jnp.float32
        ) + causal_ref[...]
        s_prefix = lax.dot_general(
            q, keys_ref[:prefix, :], contract_last, preferred_element_type=jnp.float32
        ) + bias_ref[0:1, :]
        top = jnp.maximum(
            jnp.max(s_prefix, axis=1, keepdims=True), jnp.max(s_suffix, axis=1, keepdims=True)
        )
        p_prefix = jnp.exp2((s_prefix - top) * exp2_scale)
        p_suffix = jnp.exp2((s_suffix - top) * exp2_scale)
        total = jnp.sum(p_prefix, axis=1, keepdims=True) + jnp.sum(p_suffix, axis=1, keepdims=True)
        mixed = jnp.dot(
            p_prefix.astype(jnp.bfloat16), keys_ref[:prefix, :VLAT], preferred_element_type=jnp.float32
        ) + jnp.dot(
            p_suffix.astype(jnp.bfloat16), keys_ref[prefix:, :VLAT], preferred_element_type=jnp.float32
        )
        mixed = (mixed / total).astype(jnp.bfloat16)
        w = wg_ref[:, h].reshape(VLAT, VHEAD)
        out_ref[:, h * VHEAD:(h + 1) * VHEAD] = jnp.dot(
            mixed, w, preferred_element_type=jnp.float32
        ).astype(jnp.bfloat16)


def attend(block_rows, owners, ranks, length, queries, gathered, suffix, w_all):
    heads = queries.shape[1] // LAT
    serve_n, w_rows = w_all.shape[0], w_all.shape[2]
    whole = lambda shape: pl.BlockSpec(shape, lambda i, *_: (0,) * len(shape))
    return pl.pallas_call(
        functools.partial(attend_kernel, block_rows),
        out_shape=jax.ShapeDtypeStruct((SUF, heads * VHEAD), jnp.bfloat16),
        grid_spec=pltpu.PrefetchScalarGridSpec(
            num_scalar_prefetch=3,
            grid=(heads // 2,),
            in_specs=[
                pl.BlockSpec((SUF, 2 * LAT), lambda i, *_: (0, i)),
                whole(gathered.shape),
                whole(suffix.shape),
                pl.BlockSpec((serve_n, 2, w_rows, VHEAD), lambda i, *_: (0, i, 0, 0)),
            ],
            out_specs=pl.BlockSpec((SUF, 2 * VHEAD), lambda i, *_: (0, i)),
            scratch_shapes=[
                pltpu.VMEM((KEYS, WIDE), jnp.bfloat16),
                pltpu.VMEM((8, PPAGES * PAGE), jnp.float32),
                pltpu.VMEM((SUF, SUF), jnp.float32),
            ],
        ),
        compiler_params=pltpu.CompilerParams(vmem_limit_bytes=48 * 1024 * 1024),
        name="attend",
    )(owners, ranks, length, queries, gathered, suffix, w_all)


def local(n, serve_n, queries, new_latent, pool, page_owner, page_slot, new_owner, new_slot,
          prefix_len, w_uv):
    holder = lax.axis_index("pool")
    owners = page_owner[0]
    slot_ids = page_slot[0]
    local_pages = pool[0]
    page_index = jnp.arange(PPAGES, dtype=jnp.int32)
    earlier = (page_index[None, :] < page_index[:, None]) & (owners[None, :] == owners[:, None])
    ranks = jnp.sum(earlier.astype(jnp.int32), axis=1)
    my_ranks = jnp.arange(HOT, dtype=jnp.int32)
    my_rows = (owners[None, :] == holder) & (ranks[None, :] == my_ranks[:, None])
    slot_rows = jnp.sum(jnp.where(my_rows, slot_ids[None, :], 0), axis=1)

    pages = local_pages[slot_rows].reshape(HOT, PAGE, LAT)
    latent = pages[:, :, :VLAT].reshape(HOT, PAGE, VLAT // LANES, LANES).transpose(0, 2, 1, 3)
    latent = latent.reshape(HOT, PAGE * VLAT // LANES, LANES)
    rope = pages[:, :, VLAT:].reshape(HOT, 2, PAGE // 2, ROPE).transpose(0, 2, 1, 3)
    rope = rope.reshape(HOT, PAGE // 2, LANES)
    packed = jnp.concatenate([latent, rope], axis=1).reshape(HOT * PAGE_ROWS, LANES)
    fresh = new_latent.reshape(-1, LANES)
    used = HOT * PAGE_ROWS + fresh.shape[0]
    block_rows = -(-used // 32) * 32
    filler = jnp.zeros((block_rows - used, LANES), jnp.bfloat16)
    block = jnp.concatenate([packed, fresh, filler], axis=0).reshape(2, block_rows // 2, LANES)

    gathered, w_all = exchange(n, serve_n, block, w_uv)
    by_owner = gathered.reshape(n, block_rows, LANES)
    suffix_flat = by_owner[:, HOT * PAGE_ROWS:used]
    suffix = jnp.pad(suffix_flat.reshape(SUF, LAT), ((0, 0), (0, WIDE - LAT)))
    attended = attend(
        block_rows, owners, ranks, prefix_len, queries[0],
        gathered.reshape(n * block_rows, LANES), suffix, w_all,
    )

    fresh_pages = suffix_flat.reshape(NEWP, PAGE * LAT)
    placing = (jnp.arange(SLOTS, dtype=jnp.int32)[:, None] == new_slot[0][None, :]) & (
        new_owner[0][None, :] == holder
    )
    written = jnp.dot(
        placing.astype(jnp.bfloat16), fresh_pages, preferred_element_type=jnp.float32
    ).astype(jnp.bfloat16)
    updated = jnp.where(jnp.any(placing, axis=1)[:, None], written, local_pages)
    return (attended[None], updated[None])


def solution(mesh):
    in_specs = (
        P("serve", None, "pool"),
        P("serve", "pool"),
        P("serve", "pool", None),
        P("serve", None),
        P("serve", None),
        P("serve", None),
        P("serve", None),
        P("serve"),
        P("pool", "serve", None),
    )
    out_specs = (P("serve", None, "pool"), P("serve", "pool", None))
    body = functools.partial(local, mesh.shape["pool"], mesh.shape["serve"])
    return jax.shard_map(body, mesh=mesh, in_specs=in_specs, out_specs=out_specs, check_vma=False)
```

time: 161 us -> 91.2 us (0.57); the launches traced: 159 us -> 90.7 us
  Pallas kernels: 0 us -> 72.7 us
  blocking collectives: 37.7 us -> 0 us
  matrix products: 39.7 us -> 2.97 us
  waiting for transfers between devices: 22.8 us -> 0 us
  local copies, waits for them, and re-layouts: 28.6 us -> 10.9 us
  between operations: 15 us -> 1.45 us
  other arithmetic: 14.8 us -> 2.78 us
    pallas_call x0 -> x2, Pallas kernels: none -> 72.7 us  [the longest x1 40.9 us: exchange(): pl.pallas_call(functools.partial(exchange_kernel, n, serve_n), out_shape=...]
    all_gather x1 -> x0, blocking collectives: 37.7 us -> none  [local(): suffix_all = lax.all_gather(new_latent, 'pool', axis=1, tiled=True)]
    dot_general x10 -> x0, matrix products: 37.1 us -> none  [the longest x4 13.7 us: absorb(): jnp.einsum('hqk,kv->hqv', weights.astype(jnp.bfloat16), key_rows[:, :VLAT...]
    all_gather x2 -> x0, waiting for transfers between devices: 22.8 us -> none  [the longest x1 22.8 us: local(): gathered = lax.all_gather(outgoing, 'pool', axis=0, tiled=True)]
    unnamed x32 -> x14, local copies, waits for them, and re-layouts: 10.7 us -> 3.08 us
    all_gather x1 -> x0, other arithmetic: 6.11 us -> none  [local(): suffix_all = lax.all_gather(new_latent, 'pool', axis=1, tiled=True)]
    gather x2 -> x1, local copies, waits for them, and re-layouts: 6.63 us -> 2.4 us  [local(): pages = local_pages[slot_rows].reshape(HOT, PAGE, LAT)]
    reduce_sum x6 -> x1, other arithmetic: 4.89 us -> 0.91 us  [local(): ranks = jnp.sum(earlier.astype(jnp.int32), axis=1)]
  transfers between devices with their start and end apart: 2 -> 0, of which waited for: 1 -> 0; matrix products, arithmetic and copies ran while one was open for 42% -> 0% of each run, Pallas kernels for 0% -> 0%
where the time goes in v1:
time: 91.2 us; the launch traced here: 90.7 us
  Pallas kernels  72.7 us (80%)
  local copies, waits for them, and re-layouts  10.9 us (12%)
  matrix products  2.97 us (3%)
  other arithmetic  2.78 us (3%)
  between operations  1.45 us (2%)
    pallas_call x1, Pallas kernels, exchange(): pl.pallas_call(functools.partial(exchange_kernel, n, serve_n), out_shape=...  40.9 us
    pallas_call x1, Pallas kernels, attend(): pl.pallas_call(functools.partial(attend_kernel, block_rows), out_shape=ja...  31.7 us
    unnamed x14, local copies, waits for them, and re-layouts  3.08 us
    dot_general x1, matrix products, local(): jnp.dot(placing.astype(jnp.bfloat16), fresh_pages, preferred_element_type...  2.97 us
    gather x1, local copies, waits for them, and re-layouts, local(): pages = local_pages[slot_rows].reshape(HOT, PAGE, LAT)  2.4 us
    reshape x1, local copies, waits for them, and re-layouts, local(): suffix = jnp.pad(suffix_flat.reshape(SUF, LAT), ((0, 0), (0, WIDE - LAT)))  1.96 us

profile of v1, /device:TPU:16, one launch (start us, length us, event | category | flops | bytes accessed | tf_op | source)
XLA Modules:
  0.0 90.7 jit_solution(3226496236579696852)
XLA Ops:
  0.6 0.9 %convert_reduce_fusion.rank_ref = s32[32]{0:T(128)S(1)} fusion(s32[32]{0:T(128)} %bitcast.32), kind=kLoop, calls=%fused_computation.6 | loop fusion | flops 5088 | bytes 256 | tf_op jit(solution)/shard_map/reduce_sum | solution.py:236
  1.5 0.7 compare_bitcast_fusion.1
  2.2 0.8 select_reduce_fusion
  3.0 2.4 %gather_fusion = bf16[3,36864]{1,0:T(4,128)(2,1)S(1)} fusion(bf16[12,36864]{1,0:T(8,128)(2,1)} %bitcast.34, s32[1024]{0:T(1024)S(1)} %pad_clamp_fusion), kind=kCustom, calls=%fused_computation | custom fusion | bytes 442380 | tf_op jit(solution)/shard_map/gather | solution.py:241
  5.4 0.0 copy-start.4
  5.4 0.3 reshape.56
  5.7 0.1 reshape.57
  5.9 0.1 reshape.60
  6.0 0.1 copy-done.4
  6.2 0.1 reduce
  6.3 0.1 pad.7.clone
  6.4 0.2 maximum_maximum_fusion
  6.6 0.0 copy-start.2
  6.6 1.0 %copy-done.2 = bf16[8,256,128]{2,1,0:T(8,128)(2,1)S(1)} copy-done((bf16[8,256,128]{2,1,0:T(8,128)(2,1)S(1)}, bf16[8,256,128]{2,1,0:T(8,128)(2,1)}, u32[]{:S(2)}) %copy-start.2) | copy-done | bytes 524312
  7.6 0.0 copy-start.1
  7.6 0.0 copy-start.3
  7.6 40.9 %exchange.1 = (bf16[16,2,480,128]{3,2,1,0:T(8,128)(2,1)S(1)}, bf16[2,8,256,128]{3,2,1,0:T(8,128)(2,1)S(1)}) custom-call(bf16[2,480,128]{2,1,0:T(8,128)(2,1)S(1)} %bitcast.31, bf16[8,256,128]{2,1,0:T(8,128)(2,1)S(1)} %copy-done.2), custom_call_target="tpu_custom_call" | custom-call | tf_op jit(solution)/shard_map/exchange/pallas_call | solution.py:126
  48.6 0.0 copy-start
  48.6 1.9 %copy-done = bf16[16,2,480,128]{3,2,1,0:T(8,128)(2,1)} copy-done((bf16[16,2,480,128]{3,2,1,0:T(8,128)(2,1)}, bf16[16,2,480,128]{3,2,1,0:T(8,128)(2,1)S(1)}, u32[]{:S(2)}) %copy-start) | copy-done | bytes 3932184
  50.4 0.7 slice.16
  51.2 2.0 %reshape.66 = bf16[256,576]{1,0:T(8,128)(2,1)} reshape(bf16[16,72,128]{2,1,0:T(8,128)(2,1)} %slice.16) | data formatting | bytes 589824 | tf_op jit(solution)/shard_map/reshape | solution.py:256
  53.1 1.0 %pad.4.suffix_ref = bf16[256,640]{1,0:T(8,128)(2,1)S(1)} pad(bf16[256,576]{1,0:T(8,128)(2,1)} %reshape.66, bf16[]{:T(256)} %constant.14.clone.1), padding=0_0x0_64 | pad | bytes 622594 | tf_op jit(solution)/shard_map/jit(_pad)/pad | solution.py:256
  54.8 0.0 copy-done.1
  54.8 0.0 copy-done.3
  54.8 0.0 copy-start.6
  54.8 0.0 copy-start.5
  54.8 31.7 %attend.1 = bf16[256,1024]{1,0:T(8,128)(2,1)} custom-call(s32[32]{0:T(128)S(1)} %bitcast.33, s32[32]{0:T(128)S(1)} %convert_reduce_fusion.rank_ref, s32[1]{0:T(128)S(6)} %copy.17.length_ref, bf16[256,4608]{1,0:T(8,128)(2,1)S(1)} %bitcast.30, bf16[15360,128]{1,0:T(8,128)(2,1)} %bitcast.29, bf16[256,640]{1,0:T(8,128)(2,1)S(1)} %pad.4.suffix_ref, ...), custom_call_target="tpu_custom_call" | custom-call | tf_op jit(solution)/shard_map/attend/pallas_call | solution.py:204
  86.6 1.1 %reshape.67 = bf16[4,36864]{1,0:T(4,128)(2,1)S(1)} reshape(bf16[16,72,128]{2,1,0:T(8,128)(2,1)} %slice.16) | data formatting | bytes 589824 | tf_op jit(solution)/shard_map/reshape | solution.py:262
  87.6 0.0 copy-done.6
  87.7 0.0 copy-done.5
  87.7 0.1 fusion.6
  87.8 3.0 %fusion.1 = bf16[1,12,36864]{2,1,0:T(8,128)(2,1)} fusion(bf16[4,36864]{1,0:T(4,128)(2,1)S(1)} %reshape.67, pred[12]{0:T(512)(128)(4,1)S(1)} %fusion.6, s32[4]{0:T(128)S(1)} %bitcast.43, pred[4]{0:T(512)(128)(4,1)S(1)} %compare_bitcast_fusion, bf16[1,12,36864]{2,1,0:T(8,128)(2,1)} %param.11), kind=kOutput, calls=%fused_computation.3 | convolution fusion | flops 4423776 | bytes 2064416 | tf_op jit(solution)/shard_map/dot_general | solution.py:266
  (9 shorter events, 0.1 us)
Async XLA Ops:
  5.4 0.8 copy-start.4
  6.6 1.0 %copy-start.2 = (bf16[8,256,128]{2,1,0:T(8,128)(2,1)S(1)}, bf16[8,256,128]{2,1,0:T(8,128)(2,1)}, u32[]{:S(2)}) copy-start(bf16[8,256,128]{2,1,0:T(8,128)(2,1)} %w_ref.1) | copy-start | bytes 1572868
  7.6 47.2 %copy-start.1 = (bf16[1,256,4608]{2,1,0:T(8,128)(2,1)S(1)}, bf16[1,256,4608]{2,1,0:T(8,128)(2,1)}, u32[]{:S(2)}) copy-start(bf16[1,256,4608]{2,1,0:T(8,128)(2,1)} %param.9) | copy-start | bytes 7077892
  7.6 47.2 %copy-start.3 = (s32[1,32]{1,0:T(1,128)S(1)}, s32[1,32]{1,0:T(1,128)}, u32[]{:S(2)}) copy-start(s32[1,32]{1,0:T(1,128)} %param.12) | copy-start | bytes 388
  48.6 1.9 %copy-start = (bf16[16,2,480,128]{3,2,1,0:T(8,128)(2,1)}, bf16[16,2,480,128]{3,2,1,0:T(8,128)(2,1)S(1)}, u32[]{:S(2)}) copy-start(bf16[16,2,480,128]{3,2,1,0:T(8,128)(2,1)S(1)} %get-tuple-element.4) | copy-start | bytes 11796484
  54.8 32.8 %copy-start.6 = (s32[1,4]{1,0:T(1,128)S(1)}, s32[1,4]{1,0:T(1,128)}, u32[]{:S(2)}) copy-start(s32[1,4]{1,0:T(1,128)} %param.14) | copy-start | bytes 52
  54.8 32.8 %copy-start.5 = (s32[1,4]{1,0:T(1,128)S(1)}, s32[1,4]{1,0:T(1,128)}, u32[]{:S(2)}) copy-start(s32[1,4]{1,0:T(1,128)} %param.15) | copy-start | bytes 52

commit v2 on v1

v2 whole, which is shorter than its diff:
```python
import functools

import jax
import jax.numpy as jnp
from jax import lax
from jax.experimental import pallas as pl
from jax.experimental.pallas import tpu as pltpu
from jax.sharding import PartitionSpec as P

VLAT = 512
VHEAD = 128
PAGE = 64
SUF = 256
HOT = 3
LAT = 576
PPAGES = 32
NEWP = 4
SLOTS = 12

LANES = 128
ROPE = LAT - VLAT
PAGE_ROWS = PAGE * LAT // LANES
KEYS = PPAGES * PAGE + SUF
WIDE = 640

softmax_scale = 192.0 ** (-0.5)
masked_score = -1e30
exp2_scale = softmax_scale * 1.4426950408889634

MESH = pl.DeviceIdType.MESH


def fused_kernel(n, serve_n, tokens, block_ref, w_ref, q_ref, count_ref, out_ref, suffix_ref,
                 g_ref, wg_ref, qs_ref, k_ref, stage_ref, acc_ref, top_ref, sum_ref,
                 z_send, z_recv, x_send, x_recv, y_send, y_recv, w_send, w_recv):
    depth = n // 4
    heads = q_ref.shape[1] // LAT
    half = block_ref.shape[0] // 2
    me = lax.axis_index("pool")
    core = lax.axis_index("serve")
    x = me % 2
    y = (me // 2) % 2
    z = me // 4
    x_peer = z * 4 + y * 2 + (1 - x)
    y_peer = z * 4 + (1 - y) * 2 + x

    barrier = pltpu.get_barrier_semaphore()
    for d in range(1, depth):
        there = ((z + d) % depth) * 4 + y * 2 + x
        pl.semaphore_signal(barrier, inc=1, device_id={"pool": there}, device_id_type=MESH)
    pl.semaphore_signal(barrier, inc=1, device_id={"pool": x_peer}, device_id_type=MESH)
    pl.semaphore_signal(barrier, inc=1, device_id={"pool": y_peer}, device_id_type=MESH)
    for d in range(1, serve_n):
        pl.semaphore_signal(
            barrier, inc=1, device_id={"serve": (core + d) % serve_n}, device_id_type=MESH
        )
    pl.semaphore_wait(barrier, depth + serve_n)

    started = []

    def send(src, dst, send_sem, recv_sem, device_id):
        copy = pltpu.make_async_remote_copy(
            src_ref=src, dst_ref=dst, send_sem=send_sem, recv_sem=recv_sem,
            device_id=device_id, device_id_type=MESH,
        )
        copy.start()
        started.append(copy)
        return copy

    order = []
    for d in range(1, depth // 2 + 1):
        order.append(d)
        if depth - d != d:
            order.append(depth - d)

    def base_of(d):
        return ((z - d + depth) % depth) * 4

    def part(ref, i):
        return ref.at[pl.ds(i * half, half)]

    arrivals = {}

    def spread(d):
        owner = base_of(d) + y * 2 + x
        src = block_ref if d == 0 else g_ref.at[owner]
        dst = g_ref.at[owner]
        arrivals[d] = [
            send(part(src, 0), part(dst, 0), x_send.at[d, 0], x_recv.at[d, 0], {"pool": x_peer}),
            send(part(src, 1), part(dst, 1), y_send.at[d, 0], y_recv.at[d, 0], {"pool": y_peer}),
            send(part(src, 1), part(dst, 1), x_send.at[d, 1], x_recv.at[d, 1], {"pool": x_peer}),
            send(part(src, 0), part(dst, 0), y_send.at[d, 1], y_recv.at[d, 1], {"pool": y_peer}),
        ]

    def forward(d):
        x_first, y_first, x_second, y_second = arrivals[d]
        x_first.wait_recv()
        over = part(g_ref.at[base_of(d) + y * 2 + (1 - x)], 0)
        to_y = send(over, over, y_send.at[d, 2], y_recv.at[d, 2], {"pool": y_peer})
        y_first.wait_recv()
        over = part(g_ref.at[base_of(d) + (1 - y) * 2 + x], 1)
        to_x = send(over, over, x_send.at[d, 2], x_recv.at[d, 2], {"pool": x_peer})
        arrivals[d] = [x_second, y_second, to_y, to_x]

    spread(0)
    z_copies = {}
    for d in order:
        there = ((z + d) % depth) * 4 + y * 2 + x
        z_copies[d] = send(block_ref, g_ref.at[me], z_send.at[d], z_recv.at[d], {"pool": there})
    w_copies = [
        send(w_ref, wg_ref.at[core], w_send.at[d], w_recv.at[d], {"serve": (core + d) % serve_n})
        for d in range(1, serve_n)
    ]

    pending = []

    def advance(d):
        def step():
            z_copies[d].wait_recv()
            spread(d)
        return step

    pending.append(lambda: forward(0))
    for d in order:
        pending.append(advance(d))
        pending.append(functools.partial(forward, d))

    def communicate(steps):
        for _ in range(min(steps, len(pending))):
            pending.pop(0)()

    g_ref[pl.ds(me, 1)] = block_ref[...][None]
    wg_ref[pl.ds(core, 1)] = w_ref[...][None]
    unit = jnp.where(
        lax.broadcasted_iota(jnp.int32, (SUF, WIDE - LAT), 1) == 0, 1.0, 0.0
    ).astype(jnp.bfloat16)
    for h in range(heads):
        qs_ref[h * SUF:(h + 1) * SUF, :] = jnp.concatenate(
            [q_ref[:, h * LAT:(h + 1) * LAT], unit], axis=1
        )

    lane = lax.broadcasted_iota(jnp.int32, (PAGE // 2, LANES), 1)
    line = lax.broadcasted_iota(jnp.int32, (PAGE // 2, LANES), 0)

    def unpack(d):
        def place(i, carry):
            owner = base_of(d) + i // HOT
            rank = i % HOT
            base = pl.multiple_of(rank * PAGE_ROWS, 16)
            row = pl.multiple_of(i * PAGE, PAGE)
            for c in range(VLAT // LANES):
                k_ref[pl.ds(row, PAGE), c * LANES:(c + 1) * LANES] = g_ref[
                    owner, pl.ds(base + c * PAGE, PAGE), :]
            rope = g_ref[owner, pl.ds(base + PAGE * VLAT // LANES, PAGE // 2), :].astype(jnp.float32)
            count = count_ref[owner * HOT + rank]
            swapped = jnp.concatenate([rope[:, ROPE:], rope[:, :ROPE]], axis=1)
            for k, values in enumerate((rope, swapped)):
                absent = (lane == ROPE) & (line + k * (PAGE // 2) >= count)
                tile = jnp.where(lane < ROPE, values, jnp.where(absent, masked_score, 0.0))
                k_ref[pl.ds(row + k * (PAGE // 2), PAGE // 2), VLAT:WIDE] = tile.astype(jnp.bfloat16)
            return carry

        lax.fori_loop(0, 4 * HOT, place, 0)

    tile_rows = 2 * SUF
    tiles = heads // 2
    contract_last = (((1,), (1,)), ((), ()))

    def absorb(keys_ref, low, high, first, causal):
        def tile(t, carry):
            rows = pl.ds(pl.multiple_of(t * tile_rows, tile_rows), tile_rows)
            keys = keys_ref[...]
            scores = lax.dot_general(
                qs_ref[rows, :], keys, contract_last, preferred_element_type=jnp.float32
            )
            if causal:
                row = lax.broadcasted_iota(jnp.int32, scores.shape, 0) % SUF
                col = lax.broadcasted_iota(jnp.int32, scores.shape, 1)
                scores = jnp.where(col <= row, scores, masked_score)
            top = jnp.max(scores, axis=1, keepdims=True)
            if not first:
                before = top_ref[rows, :1]
                top = jnp.maximum(top, before)
            shift = top * exp2_scale
            weights = jnp.exp2(scores * exp2_scale - shift)
            total = jnp.sum(weights, axis=1, keepdims=True)
            mixed = jnp.dot(
                weights.astype(jnp.bfloat16), keys[:, :VLAT], preferred_element_type=jnp.float32
            )
            if not first:
                rescale = jnp.exp2((before - top) * exp2_scale)
                total = total + sum_ref[rows, :1] * rescale
                mixed = mixed + acc_ref[rows, :] * rescale
            top_ref[rows, :] = jnp.broadcast_to(top, (tile_rows, LANES))
            sum_ref[rows, :] = jnp.broadcast_to(total, (tile_rows, LANES))
            acc_ref[rows, :] = mixed
            return carry

        lax.fori_loop(low, high, tile, 0)

    communicate(2)
    for k, d in enumerate([0] + order):
        while len(arrivals[d]) != 4 or (len(pending) > 2 * (len(order) - k) and pending):
            communicate(1)
        for copy in arrivals[d]:
            copy.wait_recv()
        unpack(d)
        absorb(k_ref, 0, tiles // 2, k == 0, False)
        communicate(2)
        absorb(k_ref, tiles // 2, tiles, k == 0, False)
        communicate(2)

    base = HOT * PAGE_ROWS

    def place_suffix(o, carry):
        rows = pl.ds(pl.multiple_of(o * tokens, 8), tokens)
        for c in range(VLAT // LANES):
            stage_ref[rows, c * LANES:(c + 1) * LANES] = g_ref[
                o, base + c * tokens:base + (c + 1) * tokens, :].astype(jnp.float32)
        at = base + tokens * VLAT // LANES
        rope = g_ref[o, at:at + tokens // 2, :].astype(jnp.float32)
        swapped = jnp.concatenate([rope[:, ROPE:], rope[:, :ROPE]], axis=1)
        both = jnp.concatenate([rope, swapped], axis=0)
        keep = lax.broadcasted_iota(jnp.int32, (tokens, LANES), 1) < ROPE
        stage_ref[rows, VLAT:WIDE] = jnp.where(keep, both, 0.0)
        return carry

    lax.fori_loop(0, n, place_suffix, 0)
    suffix_ref[...] = stage_ref[...].astype(jnp.bfloat16)
    absorb(suffix_ref, 0, tiles, False, True)
    for copy in w_copies:
        copy.wait_recv()
    for h in range(heads):
        rows = slice(h * SUF, (h + 1) * SUF)
        mixed = (acc_ref[rows, :] / sum_ref[rows, :1]).astype(jnp.bfloat16)
        out_ref[:, h * VHEAD:(h + 1) * VHEAD] = jnp.dot(
            mixed, wg_ref[:, h].reshape(VLAT, VHEAD), preferred_element_type=jnp.float32
        ).astype(jnp.bfloat16)
    for copy in started:
        copy.wait_send()


def fused(n, serve_n, tokens, block, w, queries, counts):
    depth = n // 4
    heads = queries.shape[1] // LAT
    dma = pltpu.SemaphoreType.DMA
    vmem = pl.BlockSpec(memory_space=pltpu.VMEM)
    return pl.pallas_call(
        functools.partial(fused_kernel, n, serve_n, tokens),
        out_shape=(
            jax.ShapeDtypeStruct((SUF, heads * VHEAD), jnp.bfloat16),
            jax.ShapeDtypeStruct((SUF, WIDE), jnp.bfloat16),
        ),
        in_specs=[vmem, vmem, vmem, pl.BlockSpec(memory_space=pltpu.SMEM)],
        out_specs=(vmem, vmem),
        scratch_shapes=[
            pltpu.VMEM((n,) + block.shape, jnp.bfloat16),
            pltpu.VMEM((serve_n,) + w.shape, jnp.bfloat16),
            pltpu.VMEM((heads * SUF, WIDE), jnp.bfloat16),
            pltpu.VMEM((4 * HOT * PAGE, WIDE), jnp.bfloat16),
            pltpu.VMEM((SUF, WIDE), jnp.float32),
            pltpu.VMEM((heads * SUF, VLAT), jnp.float32),
            pltpu.VMEM((heads * SUF, LANES), jnp.float32),
            pltpu.VMEM((heads * SUF, LANES), jnp.float32),
            dma((depth,)), dma((depth,)),
            dma((depth, 3)), dma((depth, 3)),
            dma((depth, 3)), dma((depth, 3)),
            dma((serve_n,)), dma((serve_n,)),
        ],
        compiler_params=pltpu.CompilerParams(
            collective_id=0, has_side_effects=True, vmem_limit_bytes=48 * 1024 * 1024
        ),
        name="fused",
    )(block, w, queries, counts)


def local(n, serve_n, queries, new_latent, pool, page_owner, page_slot, new_owner, new_slot,
          prefix_len, w_uv):
    holder = lax.axis_index("pool")
    owners = page_owner[0]
    slot_ids = page_slot[0]
    local_pages = pool[0]
    page_index = jnp.arange(PPAGES, dtype=jnp.int32)
    earlier = (page_index[None, :] < page_index[:, None]) & (owners[None, :] == owners[:, None])
    ranks = jnp.sum(earlier.astype(jnp.int32), axis=1)
    my_ranks = jnp.arange(HOT, dtype=jnp.int32)
    my_rows = (owners[None, :] == holder) & (ranks[None, :] == my_ranks[:, None])
    slot_rows = jnp.sum(jnp.where(my_rows, slot_ids[None, :], 0), axis=1)

    pages = local_pages[slot_rows].reshape(HOT, PAGE, LAT)
    latent = pages[:, :, :VLAT].reshape(HOT, PAGE, VLAT // LANES, LANES).transpose(0, 2, 1, 3)
    latent = latent.reshape(HOT, PAGE * VLAT // LANES, LANES)
    rope = pages[:, :, VLAT:].reshape(HOT, 2, PAGE // 2, ROPE).transpose(0, 2, 1, 3)
    rope = rope.reshape(HOT, PAGE // 2, LANES)
    packed = jnp.concatenate([latent, rope], axis=1).reshape(HOT * PAGE_ROWS, LANES)
    fresh = new_latent.reshape(-1, LAT)
    tokens = fresh.shape[0]
    fresh_latent = fresh[:, :VLAT].reshape(tokens, VLAT // LANES, LANES).transpose(1, 0, 2)
    fresh_rope = fresh[:, VLAT:].reshape(2, tokens // 2, ROPE).transpose(1, 0, 2)
    used = HOT * PAGE_ROWS + tokens * LAT // LANES
    block_rows = -(-used // 32) * 32
    filler = jnp.zeros((block_rows - used, LANES), jnp.bfloat16)
    block = jnp.concatenate(
        [packed, fresh_latent.reshape(-1, LANES), fresh_rope.reshape(-1, LANES), filler], axis=0
    )
    spots = jnp.arange(n * HOT, dtype=jnp.int32)
    held = jnp.clip(prefix_len[0] - PAGE * page_index, 0, PAGE)
    counts = jnp.sum(
        jnp.where(spots[:, None] == (owners * HOT + ranks)[None, :], held[None, :], 0), axis=1
    )
    attended, suffix = fused(n, serve_n, tokens, block, w_uv, queries[0], counts)
    fresh_pages = suffix[:, :LAT].reshape(NEWP, PAGE * LAT)
    placing = (jnp.arange(SLOTS, dtype=jnp.int32)[:, None] == new_slot[0][None, :]) & (
        new_owner[0][None, :] == holder
    )
    written = jnp.dot(
        placing.astype(jnp.bfloat16), fresh_pages, preferred_element_type=jnp.float32
    ).astype(jnp.bfloat16)
    updated = jnp.where(jnp.any(placing, axis=1)[:, None], written, local_pages)
    return (attended[None], updated[None])


def solution(mesh):
    in_specs = (
        P("serve", None, "pool"),
        P("serve", "pool"),
        P("serve", "pool", None),
        P("serve", None),
        P("serve", None),
        P("serve", None),
        P("serve", None),
        P("serve"),
        P("pool", "serve", None),
    )
    out_specs = (P("serve", None, "pool"), P("serve", "pool", None))
    body = functools.partial(local, mesh.shape["pool"], mesh.shape["serve"])
    return jax.shard_map(body, mesh=mesh, in_specs=in_specs, out_specs=out_specs, check_vma=False)
```

time: 91.2 us -> 90.3 us (level)
  local copies, waits for them, and re-layouts: 10.9 us -> 6.5 us
  other arithmetic: 2.78 us -> 5.61 us
    reshape x2 -> x5, local copies, waits for them, and re-layouts: 3.02 us -> 1.6 us  [the longest x1 1.37 us: local(): fresh_pages = suffix[:, :LAT].reshape(NEWP, PAGE * LAT)]
    unnamed x14 -> x9, local copies, waits for them, and re-layouts: 3.08 us -> 1.8 us
    pad x1 -> x0, local copies, waits for them, and re-layouts: 1 us -> none  [local(): suffix = jnp.pad(suffix_flat.reshape(SUF, LAT), ((0, 0), (0, WIDE - LAT)))]
    pallas_call x2 -> x1, Pallas kernels: 72.7 us -> 73.4 us  [fused(): pl.pallas_call(functools.partial(fused_kernel, n, serve_n, tokens), out_s...]
where the time goes in v2:
time: 90.3 us; the launch traced here: 90 us
  Pallas kernels  73.4 us (81%)
  local copies, waits for them, and re-layouts  6.5 us (7%)
  other arithmetic  5.61 us (6%)
  matrix products  2.97 us (3%)
  between operations  1.43 us (2%)
    pallas_call x1, Pallas kernels, fused(): pl.pallas_call(functools.partial(fused_kernel, n, serve_n, tokens), out_s...  73.4 us
    dot_general x1, matrix products, local(): jnp.dot(placing.astype(jnp.bfloat16), fresh_pages, preferred_element_type...  2.97 us
    gather x1, local copies, waits for them, and re-layouts, local(): pages = local_pages[slot_rows].reshape(HOT, PAGE, LAT)  2.54 us

profile of v2, /device:TPU:16, one launch (start us, length us, event | category | flops | bytes accessed | tf_op | source)
XLA Modules:
  0.0 90.0 jit_solution(1256106764767035996)
XLA Ops:
  1.3 0.7 compare_bitcast_fusion
  2.0 0.7 compare_bitcast_fusion.1
  2.6 0.9 %convert_reduce_fusion = s32[32]{0:T(128)S(1)} fusion(s32[32]{0:T(128)} %bitcast.59), kind=kLoop, calls=%fused_computation.11 | loop fusion | flops 5088 | bytes 256 | tf_op jit(solution)/shard_map/reduce_sum | solution.py:285
  3.5 0.8 select_reduce_fusion.1
  4.3 0.7 fusion.10
  5.0 0.1 select_reduce_fusion.count_ref
  5.1 0.7 fusion.6
  5.8 0.1 pad.3.clone
  5.9 0.9 reduce
  6.8 0.1 reshape.69
  6.9 0.1 reshape.73
  7.0 0.0 copy-start
  7.0 2.5 %gather_fusion = bf16[3,36864]{1,0:T(4,128)(2,1)S(1)} fusion(bf16[12,36864]{1,0:T(8,128)(2,1)} %bitcast.49, s32[1024]{0:T(1024)S(1)} %pad_clamp_fusion), kind=kCustom, calls=%fused_computation | custom fusion | bytes 442380 | tf_op jit(solution)/shard_map/gather | solution.py:290
  9.6 0.0 copy-start.1
  9.6 0.3 reshape.63
  10.0 0.1 reshape.67
  10.1 0.2 maximum_maximum_fusion.block_ref
  10.3 0.0 copy-done
  10.3 0.3 copy-done.1
  10.6 0.0 copy-start.3
  10.6 73.4 %fused.1 = (bf16[256,1024]{1,0:T(8,128)(2,1)S(1)}, bf16[256,640]{1,0:T(8,128)(2,1)S(1)}) custom-call(bf16[960,128]{1,0:T(8,128)(2,1)S(1)} %maximum_maximum_fusion.block_ref, bf16[8,256,128]{2,1,0:T(8,128)(2,1)S(1)} %copy-done.1, bf16[256,4608]{1,0:T(8,128)(2,1)S(1)} %bitcast.46, s32[48]{0:T(128)S(1)} %select_reduce_fusion.count_ref), custom_call_target="tpu_custom_call" | custom-call | tf_op jit(solution)/shard_map/fused/pallas_call | solution.py:248
  84.1 0.0 copy-start.2
  84.1 0.7 copy-done.2
  84.8 1.4 %reshape.74 = bf16[4,36864]{1,0:T(4,128)(2,1)S(1)} reshape(bf16[256,576]{1,0:T(8,128)(2,1)} %bitcast.48) | data formatting | bytes 589824 | tf_op jit(solution)/shard_map/reshape | solution.py:312
  86.2 0.0 copy-done.3
  86.2 3.0 %fusion.1 = bf16[1,12,36864]{2,1,0:T(8,128)(2,1)} fusion(bf16[4,36864]{1,0:T(4,128)(2,1)S(1)} %reshape.74, pred[12]{0:T(512)(128)(4,1)S(1)} %fusion.6, s32[4]{0:T(128)S(1)} %bitcast.58, pred[4]{0:T(512)(128)(4,1)S(1)} %compare_bitcast_fusion, bf16[1,12,36864]{2,1,0:T(8,128)(2,1)} %param.11), kind=kOutput, calls=%fused_computation.3 | convolution fusion | flops 4423776 | bytes 2064416 | tf_op jit(solution)/shard_map/dot_general | solution.py:316
  89.2 0.8 copy.27
  (13 shorter events, 0.2 us)
Async XLA Ops:
  7.0 3.3 %copy-start = (bf16[1,256,4608]{2,1,0:T(8,128)(2,1)S(1)}, bf16[1,256,4608]{2,1,0:T(8,128)(2,1)}, u32[]{:S(2)}) copy-start(bf16[1,256,4608]{2,1,0:T(8,128)(2,1)} %param.9) | copy-start | bytes 7077892
  9.6 1.0 %copy-start.1 = (bf16[8,256,128]{2,1,0:T(8,128)(2,1)S(1)}, bf16[8,256,128]{2,1,0:T(8,128)(2,1)}, u32[]{:S(2)}) copy-start(bf16[8,256,128]{2,1,0:T(8,128)(2,1)} %w_ref.1) | copy-start | bytes 1572868
  10.6 75.6 %copy-start.3 = (s32[1,4]{1,0:T(1,128)S(1)}, s32[1,4]{1,0:T(1,128)}, u32[]{:S(2)}) copy-start(s32[1,4]{1,0:T(1,128)} %param.15) | copy-start | bytes 52
  84.1 0.7 copy-start.2
